TPU v7x, 32 devices: a whole 2x2x4 slice. The times are simulated.
32 devices in a mesh: dp: 4 (over y, x), expert: 8 (over z, core).
Axes of the slice: x: 2, y: 2, z: 4, core: 2. Of those that a mesh axis runs over, the one named last changes fastest.
Arguments:
- tokens: bfloat16 [1024, 4096], P('dp', 'expert'), may hold values from -6 to 6
- routing: int32 [1024, 2], P('dp'), may hold values from 0 to 3, all different within a row; in each aligned block of 256 rows (0 to 255, 256 to 511, ...) at most 192 rows name the same one
- gate_weight: bfloat16 [4096, 4], P('expert'), may hold values from -0.09375 to 0.09375
- expert_in: bfloat16 [4, 4096, 8192], P('dp', None, 'expert'), may hold values from -0.09375 to 0.09375
- expert_out: bfloat16 [4, 8192, 4096], P('dp', 'expert'), may hold values from -0.75 to 0.75
Outputs:
- mixed: bfloat16 [1024, 4096], P('dp', 'expert')
Inputs may be any that keep to these rules, and one draw needn't show every extreme that they name: `routing`: each row names two different experts. Within the 256 rows of one group, no expert is named by more than 192 rows, a bound that some block reaches.
All inputs are finite; a program needn't handle non-finite values.
Results may differ from a plain program's by a relative error of at most 0.02.
Values may be sent and summed in bfloat16 or wider, within the bound.
A program may use at most 64 MiB of HBM per device.

v0:
```python
import functools

import jax
import jax.numpy as jnp
from jax import lax
from jax.experimental import pallas as pl
from jax.experimental.pallas import tpu as pltpu
from jax.sharding import PartitionSpec as P


def softmax_rows(logits):
    raised = jnp.exp(logits)
    return raised / jnp.sum(raised, axis=-1, keepdims=True)


def pick_chosen(softmax_all, picks):
    experts = softmax_all.shape[1]
    labels = lax.broadcasted_iota(jnp.int32, (picks.shape[0], 2, experts), 2)
    selected = labels == picks[:, :, None]
    return jnp.sum(jnp.where(selected, softmax_all[:, None, :], 0.0), axis=-1).astype(jnp.bfloat16)


def expert_rows(block_rows, weight_in, weight_out):
    sources = block_rows.shape[0]
    slots_here = block_rows.shape[1]
    width_local = block_rows.shape[2]
    flat_rows = block_rows.reshape(sources * slots_here, width_local)
    pre_act = jnp.dot(
        lax.all_gather(flat_rows, "expert", axis=1, tiled=True),
        weight_in,
        preferred_element_type=jnp.float32,
    )
    hidden = jax.nn.gelu(pre_act, approximate=True).astype(jnp.bfloat16)
    partial_out = jnp.dot(hidden, weight_out, preferred_element_type=jnp.float32)
    summed = lax.psum_scatter(
        partial_out.astype(jnp.bfloat16), "expert", scatter_dimension=1, tiled=True
    )
    return summed.reshape(sources, slots_here, width_local)


def slots_plan(tokens, routing, gate_weight, expert_in, expert_out):
    group_size = tokens.shape[0]
    width_local = tokens.shape[1]
    experts = gate_weight.shape[1]
    dp_count = lax.axis_size("dp")
    capacity = 3 * group_size // dp_count
    weight_in = expert_in[0]
    weight_out = expert_out[0]
    partial_logits = jnp.dot(tokens, gate_weight, preferred_element_type=jnp.float32)
    logits = lax.psum(partial_logits, "expert")
    chosen = pick_chosen(softmax_rows(logits), routing)
    order = jnp.concatenate([routing[:, 0], routing[:, 1]], axis=0)
    labels = lax.broadcasted_iota(jnp.int32, (2 * group_size, experts), 1)
    onehot = (labels == order[:, None]).astype(jnp.int32)
    before = jnp.cumsum(onehot, axis=0) - onehot
    slot_flat = jnp.sum(before * onehot, axis=1)
    slot_index = jnp.stack([slot_flat[:group_size], slot_flat[group_size:]], axis=1)
    target = routing * capacity + slot_index
    columns = lax.broadcasted_iota(jnp.int32, (group_size, experts * capacity), 1)
    first_hit = columns == target[:, 0:1]
    second_hit = columns == target[:, 1:2]
    assign = jnp.logical_or(first_hit, second_hit).astype(jnp.bfloat16)
    outgoing = jnp.einsum("gs,gd->sd", assign, tokens, preferred_element_type=jnp.float32)
    outgoing = outgoing.astype(jnp.bfloat16).reshape(experts, capacity, width_local)
    incoming = lax.all_to_all(outgoing, "dp", split_axis=0, concat_axis=0, tiled=True)
    processed = expert_rows(incoming, weight_in, weight_out)
    returned_rows = lax.all_to_all(processed, "dp", split_axis=0, concat_axis=0, tiled=True)
    zero_weight = jnp.zeros((), jnp.bfloat16)
    combine = jnp.where(first_hit, chosen[:, 0:1], zero_weight) + jnp.where(
        second_hit, chosen[:, 1:2], zero_weight
    )
    mixed = jnp.dot(
        combine,
        returned_rows.reshape(experts * capacity, width_local),
        preferred_element_type=jnp.float32,
    )
    return mixed.astype(jnp.bfloat16)


MESH = pl.DeviceIdType.MESH
F32 = jnp.float32
BF16 = jnp.bfloat16


def whole_kernel(
    experts,
    tok, gate_in, routes, win_hbm, wout_hbm, out,
    extra,
    xs, ex, win, wout, pre, logit, hidden, give, take, part, hop, zin,
    wsem, xs_s, xs_r, zs, zr, fs, fr, ds, dr, es, er, ps, pr, hs, hr, us, ur,
):
    dp, me = lax.axis_index("dp"), lax.axis_index("expert")
    z, k = me // 2, me % 2
    depth = lax.axis_size("expert") // 2
    group, width = tok.shape
    half = group // 2
    gx, gy = dp // 2 * 2 + 1 - dp % 2, (1 - dp // 2) * 2 + dp % 2
    gd = 3 - dp
    other = z * 2 + 1 - k
    top, low = pl.ds(0, half), pl.ds(half, half)
    peers = [(g, me) for g in (gx, gy, gd)]
    peers += [(dp, lax.rem(me + i, 2 * depth)) for i in range(1, 2 * depth)]

    def send(src, dst, s_sem, r_sem, who):
        copy = pltpu.make_async_remote_copy(src, dst, s_sem, r_sem, device_id=who, device_id_type=MESH)
        copy.start()
        started.append(copy)

    def got(ref, s_sem, r_sem):
        pltpu.make_async_remote_copy(ref, ref, s_sem, r_sem, device_id=(dp, other), device_id_type=MESH).wait_recv()

    started = []
    load_in = pltpu.make_async_copy(win_hbm.at[0], win, wsem.at[0])
    load_out = pltpu.make_async_copy(wout_hbm.at[0], wout, wsem.at[1])
    load_in.start()
    load_out.start()
    barrier = pltpu.get_barrier_semaphore()
    for who in peers:
        pl.semaphore_signal(barrier, inc=1, device_id=who, device_id_type=MESH)
    pl.semaphore_wait(barrier, len(peers))

    upper = z // 2
    near = z * (1 - upper) + (depth - 1 - z) * upper
    middle = near == 1

    def origin(s):
        seen = near if s == 0 else 1 - near if s == 1 else s
        return seen * (1 - upper) + (depth - 1 - seen) * upper

    def pass_on(block, b, to, s_sem):
        return pltpu.make_async_remote_copy(
            block, xs.at[dp, b, k], s_sem, zr.at[b], device_id=(dp, to * 2 + k), device_id_type=MESH
        )

    def forward(s):
        b = origin(s)
        block = xs.at[dp, b, k]
        to = jnp.where(b < z, z + 1, z - 1)
        return pass_on(block, b, to, zs.at[s])

    def spread(s):
        zz = origin(s)
        block = tok if s == 0 else xs.at[dp, zz, k]
        for i, (who, rows) in enumerate(((gx, top), (gy, low), (gx, low), (gy, top))):
            send(block.at[rows], xs.at[dp, zz, k, rows], xs_s.at[s, i], xs_r.at[s, i], (who, me))
        send(block, xs.at[dp, zz, k], ds.at[s, 0], dr.at[s, 0], (dp, other))

    send(tok, xs.at[dp, z, k], zs.at[0], zr.at[z], (dp, (z + 1 - 2 * (z % 2)) * 2 + k))
    crossing = pass_on(tok, z, depth - 1 - z, zs.at[depth])

    @pl.when(middle)
    def _():
        crossing.start()

    spread(0)
    wide = lax.broadcasted_iota(jnp.int32, (16, experts), 0) == lax.broadcasted_iota(jnp.int32, (16, experts), 1)
    pair = lax.broadcasted_iota(jnp.int32, (16, 2), 0) == lax.broadcasted_iota(jnp.int32, (16, 2), 1) + experts
    across = (((1,), (1,)), ((), ()))
    gate_rows = lax.dot_general(
        jnp.where(wide, 1.0, 0.0).astype(BF16), gate_in[...], across, preferred_element_type=F32
    )
    route_rows = lax.dot_general(
        jnp.where(pair, 1.0, 0.0).astype(BF16), routes[...].astype(F32).astype(BF16), across, preferred_element_type=F32
    )
    extra[...] = gate_rows.astype(BF16)
    extra[:, :group] = (gate_rows[:, :group] + route_rows).astype(BF16)
    for i, who in enumerate(peers):
        slot = dp if i < 3 else 4 + i - 3
        send(extra, ex.at[slot], es.at[i], er.at[i], who)
    xs[dp, z, k] = tok[...]
    pre[...] = jnp.zeros_like(pre)
    logit[...] = jnp.zeros_like(logit)

    def along(s):
        b = origin(s)
        got(xs.at[dp, b, k], zs.at[s], zr.at[b])

    def relay(s):
        pl.when(middle)(forward(s).start)

    def accumulate(s, g):
        zz = origin(s)
        total, score = pre[g], logit[g]
        for kk in range(2):
            away = lax.rem(me + 2 * depth - (zz * 2 + kk), 2 * depth)
            gate = ex[4 + lax.rem(away + 2 * depth - 1, 2 * depth)]
            rows = pl.ds(pl.multiple_of((zz * 2 + kk) * width, width), width)
            block = xs[g, zz, kk]
            total += jnp.dot(block, win[rows, :], preferred_element_type=F32)
            score += lax.dot_general(gate, block, (((1,), (1,)), ((), ())), preferred_element_type=F32)
        pre[g] = total
        logit[g] = score

    def absorb(s):
        for i, g in enumerate((dp, gx, gy, gd)):
            got(xs.at[g, origin(s), 1 - k], ds.at[s, i], dr.at[s, i])
        lax.fori_loop(0, 4, lambda g, carry: accumulate(s, g) or carry, 0)

    for s in range(depth):
        zz = origin(s)
        got(xs.at[gx, zz, k, top], xs_s.at[s, 0], xs_r.at[s, 0])
        send(xs.at[gx, zz, k, top], xs.at[gx, zz, k, top], fs.at[s, 0], fr.at[s, 0], (gy, me))
        got(xs.at[gy, zz, k, low], xs_s.at[s, 1], xs_r.at[s, 1])
        send(xs.at[gy, zz, k, low], xs.at[gy, zz, k, low], fs.at[s, 1], fr.at[s, 1], (gx, me))
        if s + 1 < depth:
            if s == 0:
                along(1)
                relay(1)
                pl.when(middle)(lambda: along(2))
                relay(2)
            else:
                pl.when(jnp.logical_not(middle))(functools.partial(along, s + 1))
            if s == 1:
                pl.when(middle)(lambda: along(3))
                relay(3)
            spread(s + 1)
        if s == 1:
            for i, g in enumerate((gx, gy, gd)):
                got(ex.at[g], es.at[i], er.at[i])
            for i in range(1, 2 * depth):
                got(ex.at[3 + i], es.at[2 + i], er.at[2 + i])
            ex[dp] = extra[...]
            ex[4 + 2 * depth - 1] = extra[...]
            load_in.wait()
        if s > 0:
            absorb(s - 1)
        got(xs.at[gx, zz, k, low], xs_s.at[s, 2], xs_r.at[s, 2])
        send(xs.at[gx, zz, k], xs.at[gx, zz, k], ds.at[s, 1], dr.at[s, 1], (dp, other))
        got(xs.at[gy, zz, k, top], xs_s.at[s, 3], xs_r.at[s, 3])
        send(xs.at[gy, zz, k], xs.at[gy, zz, k], ds.at[s, 2], dr.at[s, 2], (dp, other))
        got(xs.at[gd, zz, k, top], fs.at[s, 0], fr.at[s, 0])
        got(xs.at[gd, zz, k, low], fs.at[s, 1], fr.at[s, 1])
        send(xs.at[gd, zz, k], xs.at[gd, zz, k], ds.at[s, 3], dr.at[s, 3], (dp, other))

    def activate(g, carry):
        score = logit[g]
        row = lax.broadcasted_iota(jnp.int32, score.shape, 0)
        raised = jnp.where(row < experts, jnp.exp(score), 0.0)
        chance = raised / jnp.sum(raised, axis=0, keepdims=True)
        mine = jnp.sum(jnp.where(row == dp, chance, 0.0), axis=0, keepdims=True)
        picks = ex[g][:, :group].astype(F32)
        named = jnp.logical_and(jnp.logical_or(row == experts, row == experts + 1), picks == dp.astype(F32))
        hit = jnp.sum(jnp.where(named, 1.0, 0.0), axis=0, keepdims=True)
        scale = mine.astype(BF16).astype(F32) * hit
        column = jnp.transpose(jnp.broadcast_to(scale, (128, group)))[:, :1]
        acted = jax.nn.gelu(pre[g], approximate=True)
        hidden[g] = (acted * column).astype(BF16)
        return carry

    def target(s):
        return origin(depth - 1 - s)

    def product(g, zz, kk):
        cols = pl.ds(pl.multiple_of((zz * 2 + kk) * width, width), width)
        return jnp.dot(hidden[g], wout[:, cols], preferred_element_type=F32)

    def lend(s, g):
        give[s, g] = product(g, target(s), 1 - k).astype(BF16)

    def keep(s, g):
        part[s, g] = (product(g, target(s), k) + take[s, g].astype(F32)).astype(BF16)

    def for_partner(s):
        lax.fori_loop(0, 4, lambda g, carry: lend(s, g) or carry, 0)
        send(give.at[s], take.at[s], ps.at[s, 0], pr.at[s, 0], (dp, other))

    def own(s):
        got(take.at[s], ps.at[s, 0], pr.at[s, 0])
        lax.fori_loop(0, 4, lambda g, carry: keep(s, g) or carry, 0)

    hops = ((gd, top, gx), (gd, low, gy), (gx, top, gx), (gy, low, gy))

    def leave(s, i):
        g, rows, who = hops[i]
        send(part.at[s, g, rows], hop.at[s, i], hs.at[s, i], hr.at[s, i], (who, me))

    def add(s, g, rows, i):
        part[s, g, rows] = (part[s, g, rows].astype(F32) + hop[s, i].astype(F32)).astype(BF16)

    def second_hop(s):
        got(hop.at[s, 0], hs.at[s, 0], hr.at[s, 0])
        add(s, gy, top, 0)
        send(part.at[s, gy, top], hop.at[s, 4], hs.at[s, 4], hr.at[s, 4], (gy, me))
        got(hop.at[s, 1], hs.at[s, 1], hr.at[s, 1])
        add(s, gx, low, 1)
        send(part.at[s, gx, low], hop.at[s, 5], hs.at[s, 5], hr.at[s, 5], (gx, me))

    outer = z + 1 - 2 * (z % 2)
    last = depth - 1

    def line(s):
        far = jnp.where(middle, depth - 1 - z, outer) if s < 2 else outer
        slot = jnp.where(middle, last + s, s)
        return pltpu.make_async_remote_copy(
            part.at[s, dp], zin.at[slot], us.at[s], ur.at[slot], device_id=(dp, far * 2 + k), device_id_type=MESH
        )

    def settle(s):
        for i in (2, 3, 4, 5):
            got(hop.at[s, i], hs.at[s, i], hr.at[s, i])
        for rows, a, b in ((top, 2, 4), (low, 3, 5)):
            total = part[s, dp, rows].astype(F32) + hop[s, a].astype(F32) + hop[s, b].astype(F32)
            part[s, dp, rows] = total.astype(BF16)
        if s < last:
            pl.when(jnp.logical_not(middle))(line(s).start)

    def gather_in(slot):
        got(zin.at[slot], us.at[0], ur.at[slot])
        return zin[slot].astype(F32)

    def merge(s):
        @pl.when(middle)
        def _():
            came = gather_in(s if s < 2 else last)
            part[s, dp] = (part[s, dp].astype(F32) + came).astype(BF16)
            line(s).start()

    load_out.wait()
    for i, g in enumerate((dp, gx, gy, gd)):
        got(xs.at[g, zz, 1 - k], ds.at[last, i], dr.at[last, i])
        accumulate(last, g)
        activate(g, 0)
        lend(0, g)
        send(give.at[0, g], take.at[0, g], ps.at[0, i], pr.at[0, i], (dp, other))
    for i, g, ways in ((1, gx, (2,)), (2, gy, (3,)), (3, gd, (0, 1)), (0, dp, ())):
        got(take.at[0, g], ps.at[0, i], pr.at[0, i])
        keep(0, g)
        for way in ways:
            leave(0, way)
    for_partner(1)
    own(1)
    leave(1, 0)
    leave(1, 1)
    for_partner(2)
    for s in range(depth):
        second_hop(s)
        if s < last:
            leave(s + 1, 2)
            leave(s + 1, 3)
        if s + 2 < depth:
            own(s + 2)
            leave(s + 2, 0)
            leave(s + 2, 1)
        if s + 3 < depth:
            for_partner(s + 3)
        if s > 1:
            merge(s - 2)
        if s > 0:
            settle(s - 1)
    merge(last - 1)
    settle(last)

    @pl.when(middle)
    def _():
        final = part[last, dp].astype(F32) + gather_in(2) + gather_in(last + 1)
        out[...] = final.astype(BF16)

    @pl.when(jnp.logical_not(middle))
    def _():
        out[...] = (part[last, dp].astype(F32) + gather_in(last + 2)).astype(BF16)

    for s in range(last):
        line(s).wait_send()
    for copy in started:
        copy.wait_send()

    @pl.when(middle)
    def _():
        crossing.wait_send()
        for s in range(1, depth):
            forward(s).wait_send()


def tokens_plan(tokens, routing, gate_weight, expert_in, expert_out):
    group, width = tokens.shape
    nx = lax.axis_size("expert")
    depth = nx // 2
    experts = gate_weight.shape[1]
    model, inner = expert_in.shape[1:]
    half = group // 2
    vmem = pltpu.VMEM
    dma = pltpu.SemaphoreType.DMA
    return pl.pallas_call(
        functools.partial(whole_kernel, experts),
        out_shape=jax.ShapeDtypeStruct((group, width), BF16),
        in_specs=[pl.BlockSpec(memory_space=vmem)] * 3 + [pl.BlockSpec(memory_space=pl.ANY)] * 2,
        out_specs=pl.BlockSpec(memory_space=vmem),
        scratch_shapes=[
            vmem((16, width), BF16),
            vmem((4, depth, 2, group, width), BF16),
            vmem((4 + nx, 16, width), BF16),
            vmem((model, inner), BF16),
            vmem((inner, model), BF16),
            vmem((4, group, inner), F32),
            vmem((4, 16, group), F32),
            vmem((4, group, inner), BF16),
            vmem((depth, 4, group, width), BF16),
            vmem((depth, 4, group, width), BF16),
            vmem((depth, 4, group, width), BF16),
            vmem((depth, 6, half, width), BF16),
            vmem((depth + 2, group, width), BF16),
            dma((2,)),
            dma((depth, 4)), dma((depth, 4)),
            dma((depth + 1,)), dma((depth,)),
            dma((depth, 2)), dma((depth, 2)),
            dma((depth, 4)), dma((depth, 4)),
            dma((2 + nx,)), dma((2 + nx,)),
            dma((depth, 4)), dma((depth, 4)),
            dma((depth, 6)), dma((depth, 6)),
            dma((depth - 1,)), dma((depth + 2,)),
        ],
        compiler_params=pltpu.CompilerParams(
            collective_id=0, has_side_effects=True, vmem_limit_bytes=63 * 1024 * 1024
        ),
    )(tokens, gate_weight, routing, expert_in, expert_out)


def solution(mesh):
    placed = (
        P("dp", "expert"),
        P("dp", None),
        P("expert", None),
        P("dp", None, "expert"),
        P("dp", "expert", None),
    )
    body = tokens_plan if tuple(mesh.shape.values()) == (4, 8) else slots_plan
    return jax.shard_map(
        body, mesh=mesh, in_specs=placed, out_specs=P("dp", "expert"), check_vma=False
    )
```

profile of v0, /device:TPU:0, one launch (start us, length us, event | category | flops | bytes accessed | tf_op | source)
XLA Modules:
  0.0 96.1 jit_solution(17522391401533555969)
XLA Ops:
  0.0 1.5 %copy.7.routes = s32[256,2]{1,0:T(8,128)} copy(s32[256,2]{0,1:T(2,128)} %param.6) | data formatting | bytes 4096 | tf_op args[1]
  1.5 1.5 %copy.6.gate_in = bf16[512,4]{1,0:T(8,128)(2,1)} copy(bf16[512,4]{0,1:T(4,128)(2,1)} %param.7) | data formatting | bytes 8192 | tf_op args[2]
  3.0 91.5 %shard_map.55 = bf16[256,512]{1,0:T(8,128)(2,1)} custom-call(bf16[256,512]{1,0:T(8,128)(2,1)} %tok.1, bf16[512,4]{1,0:T(8,128)(2,1)} %copy.6.gate_in, s32[256,2]{1,0:T(8,128)} %copy.7.routes, bf16[1,4096,1024]{2,1,0:T(8,128)(2,1)} %win_hbm.1, bf16[1,1024,4096]{2,1,0:T(8,128)(2,1)} %wout_hbm.1), custom_call_target="tpu_custom_call" | custom-call | tf_op jit(solution)/shard_map/pallas_call | solution.py:383
  94.4 1.7 %copy.9 = bf16[256,512]{1,0:T(8,128)(2,1)} copy(bf16[256,512]{1,0:T(8,128)(2,1)} %shard_map.55) | data formatting | bytes 524288
where the time goes:
time: 96.3 us; the launch traced here: 96.1 us
  Pallas kernels  91.5 us (95%)
  local copies, waits for them, and re-layouts  4.64 us (5%)
    pallas_call x1, Pallas kernels, tokens_plan(): pl.pallas_call(functools.partial(whole_kernel, experts), out_shape=jax.Sh...  91.5 us
    unnamed x3, local copies, waits for them, and re-layouts  4.64 us

commit v1 on v0

v1 whole, which is shorter than its diff:
```python
import functools

import jax
import jax.numpy as jnp
from jax import lax
from jax.experimental import pallas as pl
from jax.experimental.pallas import tpu as pltpu
from jax.sharding import PartitionSpec as P


def softmax_rows(logits):
    raised = jnp.exp(logits)
    return raised / jnp.sum(raised, axis=-1, keepdims=True)


def pick_chosen(softmax_all, picks):
    experts = softmax_all.shape[1]
    labels = lax.broadcasted_iota(jnp.int32, (picks.shape[0], 2, experts), 2)
    selected = labels == picks[:, :, None]
    return jnp.sum(jnp.where(selected, softmax_all[:, None, :], 0.0), axis=-1).astype(jnp.bfloat16)


def expert_rows(block_rows, weight_in, weight_out):
    sources = block_rows.shape[0]
    slots_here = block_rows.shape[1]
    width_local = block_rows.shape[2]
    flat_rows = block_rows.reshape(sources * slots_here, width_local)
    pre_act = jnp.dot(
        lax.all_gather(flat_rows, "expert", axis=1, tiled=True),
        weight_in,
        preferred_element_type=jnp.float32,
    )
    hidden = jax.nn.gelu(pre_act, approximate=True).astype(jnp.bfloat16)
    partial_out = jnp.dot(hidden, weight_out, preferred_element_type=jnp.float32)
    summed = lax.psum_scatter(
        partial_out.astype(jnp.bfloat16), "expert", scatter_dimension=1, tiled=True
    )
    return summed.reshape(sources, slots_here, width_local)


def slots_plan(tokens, routing, gate_weight, expert_in, expert_out):
    group_size = tokens.shape[0]
    width_local = tokens.shape[1]
    experts = gate_weight.shape[1]
    dp_count = lax.axis_size("dp")
    capacity = 3 * group_size // dp_count
    weight_in = expert_in[0]
    weight_out = expert_out[0]
    partial_logits = jnp.dot(tokens, gate_weight, preferred_element_type=jnp.float32)
    logits = lax.psum(partial_logits, "expert")
    chosen = pick_chosen(softmax_rows(logits), routing)
    order = jnp.concatenate([routing[:, 0], routing[:, 1]], axis=0)
    labels = lax.broadcasted_iota(jnp.int32, (2 * group_size, experts), 1)
    onehot = (labels == order[:, None]).astype(jnp.int32)
    before = jnp.cumsum(onehot, axis=0) - onehot
    slot_flat = jnp.sum(before * onehot, axis=1)
    slot_index = jnp.stack([slot_flat[:group_size], slot_flat[group_size:]], axis=1)
    target = routing * capacity + slot_index
    columns = lax.broadcasted_iota(jnp.int32, (group_size, experts * capacity), 1)
    first_hit = columns == target[:, 0:1]
    second_hit = columns == target[:, 1:2]
    assign = jnp.logical_or(first_hit, second_hit).astype(jnp.bfloat16)
    outgoing = jnp.einsum("gs,gd->sd", assign, tokens, preferred_element_type=jnp.float32)
    outgoing = outgoing.astype(jnp.bfloat16).reshape(experts, capacity, width_local)
    incoming = lax.all_to_all(outgoing, "dp", split_axis=0, concat_axis=0, tiled=True)
    processed = expert_rows(incoming, weight_in, weight_out)
    returned_rows = lax.all_to_all(processed, "dp", split_axis=0, concat_axis=0, tiled=True)
    zero_weight = jnp.zeros((), jnp.bfloat16)
    combine = jnp.where(first_hit, chosen[:, 0:1], zero_weight) + jnp.where(
        second_hit, chosen[:, 1:2], zero_weight
    )
    mixed = jnp.dot(
        combine,
        returned_rows.reshape(experts * capacity, width_local),
        preferred_element_type=jnp.float32,
    )
    return mixed.astype(jnp.bfloat16)


MESH = pl.DeviceIdType.MESH
F32 = jnp.float32
BF16 = jnp.bfloat16


def whole_kernel(
    experts,
    tok, gate_in, routes, win_hbm, wout_hbm, out,
    extra,
    xs, gates, picks_of, win, wout, pre, logit, hidden, give, take, part,
    from_side, from_corner, from_pair, line_pair, line_mid,
    wsem, xy_s, xy_r, relay_s, relay_r, zp_s, zm_s, z_r, pass_s, pass_r, ds, dr,
    es, er, ep_s, em_s, ez_r, eds, edr,
    ps, pr, side_s, side_r, corner_s, corner_r, pair_s, pair_r, lp_s, lp_r, lm_s, lm_r,
):
    dp, me = lax.axis_index("dp"), lax.axis_index("expert")
    z, k = me // 2, me % 2
    depth = lax.axis_size("expert") // 2
    group, width = tok.shape
    half = group // 2
    gx, gy = dp // 2 * 2 + 1 - dp % 2, (1 - dp // 2) * 2 + dp % 2
    gd = 3 - dp
    upper = z // 2
    near = z * (1 - upper) + (depth - 1 - z) * upper
    mid, edge = near == 1, near == 0
    rows = (pl.ds(0, half), pl.ds(half, half))
    partner = (dp, z * 2 + 1 - k)

    def at(q):
        return q * (1 - upper) + (depth - 1 - q) * upper

    def slot(i):
        return at(lax.rem(near + i, depth))

    def turned(j):
        return at(j + 2 * near)

    def passed(j):
        return at(j + 2 * (1 - near))

    pair, across = (dp, at(1 - near) * 2 + k), (dp, (depth - 1 - z) * 2 + k)
    side = ((gx, me), (gy, me))
    waits = []

    def make(src, dst, s_sem, r_sem, who):
        return pltpu.make_async_remote_copy(src, dst, s_sem, r_sem, device_id=who, device_id_type=MESH)

    def send(src, dst, s_sem, r_sem, who):
        copy = make(src, dst, s_sem, r_sem, who)
        copy.start()
        waits.append((None, copy))

    def send_if(role, src, dst, s_sem, r_sem, who):
        copy = make(src, dst, s_sem, r_sem, who)
        pl.when(role)(copy.start)
        waits.append((role, copy))

    def got(ref, s_sem, r_sem):
        make(ref, ref, s_sem, r_sem, partner).wait_recv()

    load_in = pltpu.make_async_copy(win_hbm.at[0], win, wsem.at[0])
    load_out = pltpu.make_async_copy(wout_hbm.at[0], wout, wsem.at[1])
    barrier = pltpu.get_barrier_semaphore()
    for who in (partner, *side, (gd, me), pair):
        pl.semaphore_signal(barrier, inc=1, device_id=who, device_id_type=MESH)

    @pl.when(mid)
    def _():
        pl.semaphore_signal(barrier, inc=1, device_id=across, device_id_type=MESH)

    load_in.start()
    load_out.start()
    pl.semaphore_wait(barrier, 5 + near)

    def mine(i):
        return tok if i == 0 else xs.at[dp, slot(i), k]

    def direct(i, h, role=None):
        for d in range(2):
            args = (mine(i).at[rows[h]], xs.at[dp, slot(i), k, rows[h]], xy_s.at[i, d, h], xy_r.at[i, d, h], side[d])
            if role is None:
                send(*args)
            else:
                pl.when(role)(make(*args).start)

    def direct_last(h, role):
        direct(3, h, role)

    def to_pair(i, h, n, s):
        zz = slot(i)
        return make(mine(i).at[rows[h]], xs.at[dp, zz, k, rows[h]], zp_s.at[n, h], z_r.at[s, h], pair)

    def to_mid(i, h, n):
        zz = slot(i)
        return make(mine(i).at[rows[h]], xs.at[dp, zz, k, rows[h]], zm_s.at[n, h], z_r.at[n, h], across)

    def line_in(i, h):
        got(xs.at[dp, slot(i), k, rows[h]], zp_s.at[0, h], z_r.at[i - 1, h])

    def cross(i, t, g, zz):
        block = tok if i == 0 and t == 0 else xs.at[g, zz, k]
        send(block, xs.at[g, zz, k], ds.at[i, t], dr.at[i, t], partner)

    def crossed(i, t, g, zz):
        got(xs.at[g, zz, 1 - k], ds.at[i, t], dr.at[i, t])

    def sides_in(i, h):
        for d, g in enumerate((gx, gy)):
            got(xs.at[g, slot(i), k, rows[h]], xy_s.at[i, d, h], xy_r.at[i, d, h])

    def relay(j, role=None):
        zz = turned(j)
        for n, (g, who) in enumerate(((gx, side[1]), (gy, side[0]))):
            block = xs.at[g, zz, k, rows[n]]
            args = (block, block, relay_s.at[j, n], relay_r.at[j, n], who)
            if role is None:
                send(*args)
            else:
                pl.when(role)(make(*args).start)

    def corner_in(j):
        zz = turned(j)
        for h in range(2):
            block = xs.at[gd, zz, k, rows[h]]
            got(block, relay_s.at[j, h], relay_r.at[j, h])
            send(block, block, pass_s.at[j, h], pass_r.at[j, h], pair)
        cross(j, 3, gd, zz)

    def passed_in(j, h):
        got(xs.at[gd, passed(j), k, rows[h]], pass_s.at[j, h], pass_r.at[j, h])

    own_line = 2 - 2 * near
    for h in range(2):
        first = to_pair(0, h, 0, own_line)
        first.start()
        waits.append((None, first))
        second = to_mid(0, h, 0)
        pl.when(mid)(second.start)
        waits.append((mid, second))
        direct(0, h)
    cross(0, 0, dp, z)

    wide = lax.broadcasted_iota(jnp.int32, (8, experts), 0) == lax.broadcasted_iota(jnp.int32, (8, experts), 1)
    both = lax.broadcasted_iota(jnp.int32, (8, 2), 0) == lax.broadcasted_iota(jnp.int32, (8, 2), 1) + experts
    gate_rows = jnp.dot(jnp.where(wide, 1.0, 0.0).astype(BF16), gate_in[...], preferred_element_type=F32)
    route_rows = jnp.dot(
        jnp.where(both, 1.0, 0.0).astype(BF16), routes[...].astype(F32).astype(BF16), preferred_element_type=F32
    )
    extra[...] = gate_rows.astype(BF16)
    extra[:, :group] = (gate_rows[:, :group] + route_rows).astype(BF16)
    for i, who in enumerate((*side, (gd, me))):
        send(extra, picks_of.at[dp], es.at[i], er.at[i], who)
    send(extra, gates.at[z, k], ep_s.at[0], ez_r.at[own_line], pair)
    send_if(mid, extra, gates.at[z, k], em_s.at[0], ez_r.at[0], across)
    send(extra, gates.at[z, k], eds.at[0], edr.at[0], partner)
    picks_of[dp] = extra[...]
    gates[z, k] = extra[...]
    xs[dp, z, k] = tok[...]
    pre[...] = jnp.zeros_like(pre)
    logit[...] = jnp.zeros_like(logit)

    def gate_in_line(i):
        zz = slot(i)
        got(gates.at[zz, k], ep_s.at[0], ez_r.at[i - 1])
        send(gates.at[zz, k], gates.at[zz, k], eds.at[i], edr.at[i], partner)

    def gate_ready(i):
        got(gates.at[slot(i), 1 - k], eds.at[i], edr.at[i])

    def accumulate(g, zz):
        total, score = pre[g], logit[g]
        for kk in range(2):
            strip = pl.ds(pl.multiple_of((zz * 2 + kk) * width, width), width)
            block = xs[g, zz, kk]
            total += jnp.dot(block, win[strip, :], preferred_element_type=F32)
            score += lax.dot_general(gates[zz, kk], block, (((1,), (1,)), ((), ())), preferred_element_type=F32)
        pre[g] = total
        logit[g] = score

    def choose(c, options):
        chosen = options[-1]
        for n in range(len(options) - 2, -1, -1):
            chosen = jnp.where(c == n, options[n], chosen)
        return chosen

    def several(count, fn):
        lax.fori_loop(0, count, lambda c, carry: fn(c) or carry, 0)

    def absorb(*which):
        for i, t, g, zz in which:
            crossed(i, t, g, zz)
        gs, zs = [w[2] for w in which], [w[3] for w in which]
        several(len(which), lambda c: accumulate(choose(c, gs), choose(c, zs)))

    def from_own(i):
        return (i, 0, dp, slot(i))

    def from_x(i):
        return (i, 1, gx, slot(i))

    def from_y(i):
        return (i, 2, gy, slot(i))

    def from_turned(j):
        return (j, 3, gd, turned(j))

    def from_passed(j):
        return (2 + j, 3, gd, passed(j))

    def forward(i, h, n, s):
        copy = to_pair(i, h, n, s)
        pl.when(mid)(copy.start)
        waits.append((mid, copy))

    def outward(h):
        copy = to_mid(3, h, 1)

        @pl.when(mid)
        def _():
            line_in(3, h)
            copy.start()

        waits.append((mid, copy))

    def cross_sides(i):
        cross(i, 1, gx, slot(i))
        cross(i, 2, gy, slot(i))

    for h in range(2):
        line_in(1, h)
        forward(1, h, 1, 1)
        direct(1, h)
        outward(h)
        sides_in(0, h)
    cross_sides(0)
    cross(1, 0, dp, slot(1))
    gate_in_line(1)
    send_if(mid, gates.at[slot(1), k], gates.at[slot(1), k], ep_s.at[1], ez_r.at[1], pair)
    gate_line_3 = make(gates.at[slot(3), k], gates.at[slot(3), k], em_s.at[1], ez_r.at[1], across)

    @pl.when(mid)
    def _():
        got(gates.at[slot(3), k], ep_s.at[0], ez_r.at[2])
        gate_line_3.start()

    waits.append((mid, gate_line_3))
    for i, g in enumerate((gx, gy, gd)):
        got(picks_of.at[g], es.at[i], er.at[i])
    load_in.wait()
    gate_ready(0)
    absorb(from_own(0))
    line_in(2, 0)
    forward(2, 0, 2, 2)
    direct(2, 0)
    sides_in(1, 0)
    absorb(from_x(0))
    line_in(2, 1)
    forward(2, 1, 2, 2)
    gate_in_line(2)
    send_if(mid, gates.at[slot(2), k], gates.at[slot(2), k], ep_s.at[2], ez_r.at[2], pair)
    sides_in(1, 1)
    relay(0)
    direct(2, 1)
    relay(1, edge)
    cross_sides(1)
    cross(2, 0, dp, slot(2))
    gate_ready(1)
    absorb(from_y(0), from_own(1))
    sides_in(2, 0)

    @pl.when(edge)
    def _():
        line_in(3, 0)
        direct_last(0, True)

    absorb(from_x(1))

    @pl.when(edge)
    def _():
        got(gates.at[slot(3), k], ep_s.at[0], ez_r.at[2])

    send(gates.at[slot(3), k], gates.at[slot(3), k], eds.at[3], edr.at[3], partner)
    corner_in(0)

    @pl.when(edge)
    def _():
        line_in(3, 1)
        direct_last(1, True)

    gate_ready(2)
    absorb(from_y(1))
    sides_in(2, 1)
    relay(1, mid)
    direct(3, 0, mid)
    direct(3, 1, mid)
    cross_sides(2)
    cross(3, 0, dp, slot(3))
    absorb(from_turned(0), from_own(2))
    passed_in(0, 0)
    corner_in(1)
    passed_in(0, 1)
    cross(2, 3, gd, passed(0))
    gate_ready(3)
    absorb(from_x(2), from_y(2))
    sides_in(3, 0)
    passed_in(1, 0)
    absorb(from_turned(1), from_passed(0), from_own(3))
    sides_in(3, 1)
    cross_sides(3)
    passed_in(1, 1)
    cross(3, 3, gd, passed(1))
    for h in range(2):
        for d in range(2):
            waits.append((None, make(mine(3).at[rows[h]], mine(3).at[rows[h]], xy_s.at[3, d, h], xy_r.at[3, d, h], side[d])))
        waits.append((None, make(mine(3).at[rows[h]], mine(3).at[rows[h]], relay_s.at[1, h], relay_r.at[1, h], side[0])))

    def activate(g):
        score = logit[g]
        row = lax.broadcasted_iota(jnp.int32, score.shape, 0)
        raised = jnp.where(row < experts, jnp.exp(score), 0.0)
        chance = raised / jnp.sum(raised, axis=0, keepdims=True)
        own = jnp.sum(jnp.where(row == dp, chance, 0.0), axis=0, keepdims=True)
        picks = picks_of[g][:, :group].astype(F32)
        named = jnp.logical_and(jnp.logical_or(row == experts, row == experts + 1), picks == dp.astype(F32))
        hit = jnp.sum(jnp.where(named, 1.0, 0.0), axis=0, keepdims=True)
        scale = own.astype(BF16).astype(F32) * hit
        column = jnp.transpose(jnp.broadcast_to(scale, (128, group)))[:, :1]
        acted = jax.nn.gelu(pre[g], approximate=True)
        hidden[g] = (acted * column).astype(BF16)

    def product(g, zz, kk):
        cols = pl.ds(pl.multiple_of((zz * 2 + kk) * width, width), width)
        return jnp.dot(hidden[g], wout[:, cols], preferred_element_type=F32)

    order = [
        (gx, slot(3)), (gy, slot(3)), (gd, passed(1)),
        (gx, slot(2)), (gy, slot(2)), (gd, passed(0)), (gd, turned(1)),
        (dp, slot(3)), (gd, turned(0)),
        (gx, slot(1)), (gy, slot(1)), (dp, slot(2)),
        (dp, slot(1)), (gx, slot(0)), (gy, slot(0)), (dp, slot(0)),
    ]

    def lend(n, g, zz):
        give[zz, g] = product(g, zz, 1 - k).astype(BF16)
        make(give.at[zz, g], take.at[zz, g], ps.at[n], pr.at[n], partner).start()

    def keep(g, zz):
        part[zz, g] = (product(g, zz, k) + take[zz, g].astype(F32)).astype(BF16)

    def lend_all(lo, hi):
        gs, zs = [w[0] for w in order[lo:hi]], [w[1] for w in order[lo:hi]]
        several(hi - lo, lambda c: lend(lo + c, choose(c, gs), choose(c, zs)))

    def taken(n):
        g, zz = order[n]
        got(take.at[zz, g], ps.at[n], pr.at[n])

    def keep_all(lo, hi):
        for n in range(lo, hi):
            taken(n)
        gs, zs = [w[0] for w in order[lo:hi]], [w[1] for w in order[lo:hi]]
        several(hi - lo, lambda c: keep(choose(c, gs), choose(c, zs)))

    for n in range(len(order)):
        g, zz = order[n]
        waits.append((None, make(give.at[zz, g], take.at[zz, g], ps.at[n], pr.at[n], partner)))

    def to_side(i, d, h):
        g = (gx, gy)[d]
        send(part.at[slot(i), g, rows[h]], from_side.at[i, d, h], side_s.at[i, d, h], side_r.at[i, d, h], side[d])

    def to_corner(j, h):
        zz = turned(j)
        got(from_pair.at[j, h], pair_s.at[j, h], pair_r.at[j, h])
        part[zz, gd, rows[h]] = (part[zz, gd, rows[h]].astype(F32) + from_pair[j, h].astype(F32)).astype(BF16)
        send(part.at[zz, gd, rows[h]], from_corner.at[j, h], corner_s.at[j, h], corner_r.at[j, h], side[h])

    def corner_add(j):
        zz = turned(j)
        for h, g in ((0, gy), (1, gx)):
            got(from_corner.at[j, h], corner_s.at[j, h], corner_r.at[j, h])
            part[zz, g, rows[h]] = (part[zz, g, rows[h]].astype(F32) + from_corner[j, h].astype(F32)).astype(BF16)

    def send_passed(j):
        zz = passed(j)
        for h in range(2):
            send(part.at[zz, gd, rows[h]], from_pair.at[j, h], pair_s.at[j, h], pair_r.at[j, h], pair)

    def gathered(i, h):
        total = part[slot(i), dp, rows[h]].astype(F32)
        for d in range(2):
            got(from_side.at[i, d, h], side_s.at[i, d, h], side_r.at[i, d, h])
            total += from_side[i, d, h].astype(F32)
        return total

    def line_pair_in(n, h):
        got(line_pair.at[n, h], lp_s.at[0, h], lp_r.at[n, h])
        return line_pair[n, h].astype(F32)

    def line_mid_in(n, h):
        got(line_mid.at[n, h], lm_s.at[0, h], lm_r.at[n, h])
        return line_mid[n, h].astype(F32)

    def line_to_pair(i, h, n):
        return make(part.at[slot(i), dp, rows[h]], line_pair.at[n, h], lp_s.at[n, h], lp_r.at[n, h], pair)

    def line_to_mid(i, h, n):
        return make(part.at[slot(i), dp, rows[h]], line_mid.at[n, h], lm_s.at[n, h], lm_r.at[n, h], across)

    def settle(i):
        for h in range(2):
            total = gathered(i, h)
            zz = slot(i)
            to_pair_copy = line_to_pair(i, h, i - 1)

            @pl.when(edge)
            def _():
                part[zz, dp, rows[h]] = total.astype(BF16)
                to_pair_copy.start()

            waits.append((edge, to_pair_copy))
            if i == 3:

                @pl.when(mid)
                def _():
                    part[zz, dp, rows[h]] = total.astype(BF16)
            else:
                copy = line_to_mid(i, h, 2 - i)

                @pl.when(mid)
                def _():
                    part[zz, dp, rows[h]] = (total + line_pair_in(i, h)).astype(BF16)
                    copy.start()

                waits.append((mid, copy))

    def outer():
        for h in range(2):
            copy = line_to_pair(3, h, 0)

            @pl.when(mid)
            def _():
                zz = slot(3)
                came = line_mid_in(0, h)
                part[zz, dp, rows[h]] = (part[zz, dp, rows[h]].astype(F32) + came).astype(BF16)
                copy.start()

            waits.append((mid, copy))

    load_out.wait()
    for n, which in enumerate((from_x(3), from_y(3), from_passed(1))):
        absorb(which)
        activate(which[2])
        lend(n, *order[n])
    keep_all(0, 1)
    for h in range(2):
        to_side(3, 0, h)
    keep_all(1, 2)
    for h in range(2):
        to_side(3, 1, h)
    keep_all(2, 3)
    send_passed(1)
    activate(dp)
    lend_all(3, 7)
    keep_all(3, 7)
    to_side(2, 0, 0)
    to_side(2, 1, 1)
    send_passed(0)
    for h in range(2):
        to_corner(1, h)
    lend_all(7, 9)
    keep_all(7, 9)
    settle(3)
    for h in range(2):
        to_corner(0, h)
    lend_all(9, 12)
    pl.when(mid)(functools.partial(corner_add, 1))
    to_side(2, 0, 1)
    to_side(2, 1, 0)
    keep_all(9, 12)
    pl.when(edge)(functools.partial(corner_add, 1))
    to_side(1, 0, 0)
    to_side(1, 1, 1)
    lend_all(12, 16)
    pl.when(mid)(functools.partial(corner_add, 0))
    to_side(1, 0, 1)
    to_side(1, 1, 0)
    settle(2)
    keep_all(12, 16)
    pl.when(edge)(functools.partial(corner_add, 0))
    for h in range(2):
        to_side(0, 0, h)
        to_side(0, 1, h)
    settle(1)
    outer()
    for h in range(2):
        total = gathered(0, h)

        @pl.when(mid)
        def _():
            out[rows[h]] = (total + line_pair_in(0, h) + line_mid_in(1, h)).astype(BF16)

        @pl.when(edge)
        def _():
            out[rows[h]] = (total + line_pair_in(0, h)).astype(BF16)

    for role, copy in waits:
        if role is None:
            copy.wait_send()
        else:
            pl.when(role)(copy.wait_send)


def tokens_plan(tokens, routing, gate_weight, expert_in, expert_out):
    group, width = tokens.shape
    depth = lax.axis_size("expert") // 2
    experts = gate_weight.shape[1]
    model, inner = expert_in.shape[1:]
    half = group // 2
    vmem = pltpu.VMEM
    dma = pltpu.SemaphoreType.DMA
    return pl.pallas_call(
        functools.partial(whole_kernel, experts),
        out_shape=jax.ShapeDtypeStruct((group, width), BF16),
        in_specs=[pl.BlockSpec(memory_space=vmem)] * 3 + [pl.BlockSpec(memory_space=pl.ANY)] * 2,
        out_specs=pl.BlockSpec(memory_space=vmem),
        scratch_shapes=[
            vmem((8, width), BF16),
            vmem((4, depth, 2, group, width), BF16),
            vmem((depth, 2, 8, width), BF16),
            vmem((4, 8, width), BF16),
            vmem((model, inner), BF16),
            vmem((inner, model), BF16),
            vmem((4, group, inner), F32),
            vmem((4, 8, group), F32),
            vmem((4, group, inner), BF16),
            vmem((depth, 4, group, width), BF16),
            vmem((depth, 4, group, width), BF16),
            vmem((depth, 4, group, width), BF16),
            vmem((depth, 2, 2, half, width), BF16),
            vmem((2, 2, half, width), BF16),
            vmem((2, 2, half, width), BF16),
            vmem((3, 2, half, width), BF16),
            vmem((2, 2, half, width), BF16),
            dma((2,)),
            dma((depth, 2, 2)), dma((depth, 2, 2)),
            dma((2, 2)), dma((2, 2)),
            dma((3, 2)), dma((2, 2)), dma((3, 2)),
            dma((2, 2)), dma((2, 2)),
            dma((depth, 4)), dma((depth, 4)),
            dma((3,)), dma((3,)),
            dma((3,)), dma((2,)), dma((3,)),
            dma((depth,)), dma((depth,)),
            dma((4 * depth,)), dma((4 * depth,)),
            dma((depth, 2, 2)), dma((depth, 2, 2)),
            dma((2, 2)), dma((2, 2)),
            dma((2, 2)), dma((2, 2)),
            dma((3, 2)), dma((3, 2)),
            dma((2, 2)), dma((2, 2)),
        ],
        compiler_params=pltpu.CompilerParams(
            collective_id=0, has_side_effects=True, vmem_limit_bytes=63 * 1024 * 1024
        ),
    )(tokens, gate_weight.T, routing.T, expert_in, expert_out)


def solution(mesh):
    placed = (
        P("dp", "expert"),
        P("dp", None),
        P("expert", None),
        P("dp", None, "expert"),
        P("dp", "expert", None),
    )
    body = tokens_plan if tuple(mesh.shape.values()) == (4, 8) else slots_plan
    return jax.shard_map(
        body, mesh=mesh, in_specs=placed, out_specs=P("dp", "expert"), check_vma=False
    )
```

time: 96.3 us -> 83.5 us (0.87)
  Pallas kernels: 91.5 us -> 81.6 us
  local copies, waits for them, and re-layouts: 4.64 us -> 1.67 us
    pallas_call x1, Pallas kernels: 91.5 us -> 81.6 us  [tokens_plan(): pl.pallas_call(functools.partial(whole_kernel, experts), out_shape=jax.Sh...]
    unnamed x3 -> x1, local copies, waits for them, and re-layouts: 4.64 us -> 1.67 us
where the time goes in v1:
time: 83.5 us; the launch traced here: 83.3 us
  Pallas kernels  81.6 us (98%)
  local copies, waits for them, and re-layouts  1.67 us (2%)
    pallas_call x1, Pallas kernels, tokens_plan(): pl.pallas_call(functools.partial(whole_kernel, experts), out_shape=jax.Sh...  81.6 us
    unnamed x1, local copies, waits for them, and re-layouts  1.67 us

profile of v1, /device:TPU:0, one launch (start us, length us, event | category | flops | bytes accessed | tf_op | source)
XLA Modules:
  0.0 83.3 jit_solution(11994841248264767456)
XLA Ops:
  0.0 81.6 %shard_map.55 = bf16[256,512]{1,0:T(8,128)(2,1)} custom-call(bf16[256,512]{1,0:T(8,128)(2,1)} %tok.1, bf16[4,512]{1,0:T(4,128)(2,1)} %bitcast.2, s32[2,256]{1,0:T(2,128)} %bitcast.3, bf16[1,4096,1024]{2,1,0:T(8,128)(2,1)} %win_hbm.1, bf16[1,1024,4096]{2,1,0:T(8,128)(2,1)} %wout_hbm.1), custom_call_target="tpu_custom_call" | custom-call | tf_op jit(solution)/shard_map/pallas_call | solution.py:601
  81.6 1.7 %copy.7 = bf16[256,512]{1,0:T(8,128)(2,1)} copy(bf16[256,512]{1,0:T(8,128)(2,1)} %shard_map.55) | data formatting | bytes 524288

commit v2 on v1

--- a/solution.py
+++ b/solution.py
@@ -84,18 +84,18 @@
 
 def whole_kernel(
     experts,
-    tok, gate_in, routes, win_hbm, wout_hbm, out,
-    extra,
+    tok_hbm, gate_hbm, routes_hbm, win_hbm, wout_hbm, out,
+    extra, gate_in, routes,
     xs, gates, picks_of, win, wout, pre, logit, hidden, give, take, part,
     from_side, from_corner, from_pair, line_pair, line_mid,
     wsem, xy_s, xy_r, relay_s, relay_r, zp_s, zm_s, z_r, pass_s, pass_r, ds, dr,
     es, er, ep_s, em_s, ez_r, eds, edr,
-    ps, pr, side_s, side_r, corner_s, corner_r, pair_s, pair_r, lp_s, lp_r, lm_s, lm_r,
+    ps, pr, hs, hr, ths, thr, side_s, side_r, corner_s, corner_r, pair_s, pair_r, lp_s, lp_r, lm_s, lm_r,
 ):
     dp, me = lax.axis_index("dp"), lax.axis_index("expert")
     z, k = me // 2, me % 2
     depth = lax.axis_size("expert") // 2
-    group, width = tok.shape
+    group, width = tok_hbm.shape
     half = group // 2
     gx, gy = dp // 2 * 2 + 1 - dp % 2, (1 - dp // 2) * 2 + dp % 2
     gd = 3 - dp
@@ -137,6 +137,11 @@
     def got(ref, s_sem, r_sem):
         make(ref, ref, s_sem, r_sem, partner).wait_recv()
 
+    own = xs.at[dp, z, k]
+    small = [
+        pltpu.make_async_copy(src, dst, wsem.at[2 + i])
+        for i, (src, dst) in enumerate(((tok_hbm, own), (gate_hbm, gate_in), (routes_hbm, routes)))
+    ]
     load_in = pltpu.make_async_copy(win_hbm.at[0], win, wsem.at[0])
     load_out = pltpu.make_async_copy(wout_hbm.at[0], wout, wsem.at[1])
     barrier = pltpu.get_barrier_semaphore()
@@ -147,23 +152,30 @@
     def _():
         pl.semaphore_signal(barrier, inc=1, device_id=across, device_id_type=MESH)
 
-    load_in.start()
-    load_out.start()
+    for copy in (*small, load_in, load_out):
+        copy.start()
     pl.semaphore_wait(barrier, 5 + near)
+    small[0].wait()
 
     def mine(i):
-        return tok if i == 0 else xs.at[dp, slot(i), k]
-
-    def direct(i, h, role=None):
-        for d in range(2):
-            args = (mine(i).at[rows[h]], xs.at[dp, slot(i), k, rows[h]], xy_s.at[i, d, h], xy_r.at[i, d, h], side[d])
+        return own if i == 0 else xs.at[dp, slot(i), k]
+
+    def span(h):
+        return pl.ds(pl.multiple_of(h * half, half), half)
+
+    def turn(i, d, h):
+        return h + near * (1 - 2 * h) if i == 2 and d == 1 else h
+
+    def direct(i, h, role=None, ways=(0, 1)):
+        for d in ways:
+            hh = turn(i, d, h)
+            copy = make(
+                mine(i).at[span(hh)], xs.at[dp, slot(i), k, span(hh)], xy_s.at[i, d, hh], xy_r.at[i, d, hh], side[d]
+            )
             if role is None:
-                send(*args)
+                copy.start()
             else:
-                pl.when(role)(make(*args).start)
-
-    def direct_last(h, role):
-        direct(3, h, role)
+                pl.when(role)(copy.start)
 
     def to_pair(i, h, n, s):
         zz = slot(i)
@@ -177,25 +189,31 @@
         got(xs.at[dp, slot(i), k, rows[h]], zp_s.at[0, h], z_r.at[i - 1, h])
 
     def cross(i, t, g, zz):
-        block = tok if i == 0 and t == 0 else xs.at[g, zz, k]
+        block = xs.at[g, zz, k]
         send(block, xs.at[g, zz, k], ds.at[i, t], dr.at[i, t], partner)
 
     def crossed(i, t, g, zz):
         got(xs.at[g, zz, 1 - k], ds.at[i, t], dr.at[i, t])
 
+    def cross_half(n, h, g, zz):
+        block = xs.at[g, zz, k, rows[h]]
+        send(block, block, hs.at[n, h], hr.at[n, h], partner)
+
     def sides_in(i, h):
         for d, g in enumerate((gx, gy)):
-            got(xs.at[g, slot(i), k, rows[h]], xy_s.at[i, d, h], xy_r.at[i, d, h])
-
-    def relay(j, role=None):
+            hh = turn(i, d, h)
+            got(xs.at[g, slot(i), k, span(hh)], xy_s.at[i, d, hh], xy_r.at[i, d, hh])
+
+    def relay(j, role=None, ways=(0, 1)):
         zz = turned(j)
-        for n, (g, who) in enumerate(((gx, side[1]), (gy, side[0]))):
+        for n in ways:
+            g, who = ((gx, side[1]), (gy, side[0]))[n]
             block = xs.at[g, zz, k, rows[n]]
-            args = (block, block, relay_s.at[j, n], relay_r.at[j, n], who)
+            copy = make(block, block, relay_s.at[j, n], relay_r.at[j, n], who)
             if role is None:
-                send(*args)
+                copy.start()
             else:
-                pl.when(role)(make(*args).start)
+                pl.when(role)(copy.start)
 
     def corner_in(j):
         zz = turned(j)
@@ -219,6 +237,8 @@
         direct(0, h)
     cross(0, 0, dp, z)
 
+    small[1].wait()
+    small[2].wait()
     wide = lax.broadcasted_iota(jnp.int32, (8, experts), 0) == lax.broadcasted_iota(jnp.int32, (8, experts), 1)
     both = lax.broadcasted_iota(jnp.int32, (8, 2), 0) == lax.broadcasted_iota(jnp.int32, (8, 2), 1) + experts
     gate_rows = jnp.dot(jnp.where(wide, 1.0, 0.0).astype(BF16), gate_in[...], preferred_element_type=F32)
@@ -234,7 +254,6 @@
     send(extra, gates.at[z, k], eds.at[0], edr.at[0], partner)
     picks_of[dp] = extra[...]
     gates[z, k] = extra[...]
-    xs[dp, z, k] = tok[...]
     pre[...] = jnp.zeros_like(pre)
     logit[...] = jnp.zeros_like(logit)
 
@@ -330,29 +349,35 @@
     absorb(from_own(0))
     line_in(2, 0)
     forward(2, 0, 2, 2)
-    direct(2, 0)
+    direct(2, 0, None, (0,))
+    direct(2, 0, edge, (1,))
     sides_in(1, 0)
+    relay(0, None, (0,))
     absorb(from_x(0))
     line_in(2, 1)
     forward(2, 1, 2, 2)
+    direct(2, 0, mid, (1,))
     gate_in_line(2)
     send_if(mid, gates.at[slot(2), k], gates.at[slot(2), k], ep_s.at[2], ez_r.at[2], pair)
     sides_in(1, 1)
-    relay(0)
+    relay(0, None, (1,))
     direct(2, 1)
     relay(1, edge)
     cross_sides(1)
     cross(2, 0, dp, slot(2))
     gate_ready(1)
-    absorb(from_y(0), from_own(1))
+    absorb(from_y(0))
     sides_in(2, 0)
+    relay(1, mid)
+    direct(3, 0, mid)
+    direct(3, 1, mid)
 
     @pl.when(edge)
     def _():
         line_in(3, 0)
-        direct_last(0, True)
-
-    absorb(from_x(1))
+        direct(3, 0, True)
+
+    absorb(from_own(1), from_x(1))
 
     @pl.when(edge)
     def _():
@@ -364,48 +389,57 @@
     @pl.when(edge)
     def _():
         line_in(3, 1)
-        direct_last(1, True)
-
+        direct(3, 1, True)
+
+    cross(3, 0, dp, slot(3))
     gate_ready(2)
-    absorb(from_y(1))
+    absorb(from_y(1), from_own(2))
     sides_in(2, 1)
-    relay(1, mid)
-    direct(3, 0, mid)
-    direct(3, 1, mid)
     cross_sides(2)
-    cross(3, 0, dp, slot(3))
-    absorb(from_turned(0), from_own(2))
+    gate_ready(3)
+    absorb(from_turned(0))
+    absorb(from_x(2))
     passed_in(0, 0)
+    absorb(from_y(2))
     corner_in(1)
     passed_in(0, 1)
     cross(2, 3, gd, passed(0))
-    gate_ready(3)
-    absorb(from_x(2), from_y(2))
+    absorb(from_own(3))
     sides_in(3, 0)
-    passed_in(1, 0)
-    absorb(from_turned(1), from_passed(0), from_own(3))
-    sides_in(3, 1)
-    cross_sides(3)
-    passed_in(1, 1)
-    cross(3, 3, gd, passed(1))
-    for h in range(2):
+    cross_half(0, 0, gx, slot(3))
+    cross_half(1, 0, gy, slot(3))
+    absorb(from_turned(1), from_passed(0))
+    for n in range(2 * depth):
         for d in range(2):
-            waits.append((None, make(mine(3).at[rows[h]], mine(3).at[rows[h]], xy_s.at[3, d, h], xy_r.at[3, d, h], side[d])))
-        waits.append((None, make(mine(3).at[rows[h]], mine(3).at[rows[h]], relay_s.at[1, h], relay_r.at[1, h], side[0])))
-
-    def activate(g):
-        score = logit[g]
+            waits.append((None, make(own.at[rows[0]], own.at[rows[0]], xy_s.at[n // 2, d, n % 2], xy_r.at[0, 0, 0], side[d])))
+    for n in range(4):
+        waits.append((None, make(own.at[rows[0]], own.at[rows[0]], relay_s.at[n // 2, n % 2], relay_r.at[0, 0], side[0])))
+
+    def accumulate_half(g, zz, h):
+        lanes = slice(h * half, h * half + half)
+        total, score = pre[g, rows[h]], logit[g, :, lanes]
+        for kk in range(2):
+            strip = pl.ds(pl.multiple_of((zz * 2 + kk) * width, width), width)
+            block = xs[g, zz, kk, rows[h]]
+            total += jnp.dot(block, win[strip, :], preferred_element_type=F32)
+            score += lax.dot_general(gates[zz, kk], block, (((1,), (1,)), ((), ())), preferred_element_type=F32)
+        pre[g, rows[h]] = total
+        logit[g, :, lanes] = score
+
+    def activate(g, h):
+        lanes = slice(h * half, h * half + half)
+        score = logit[g, :, lanes]
         row = lax.broadcasted_iota(jnp.int32, score.shape, 0)
         raised = jnp.where(row < experts, jnp.exp(score), 0.0)
         chance = raised / jnp.sum(raised, axis=0, keepdims=True)
-        own = jnp.sum(jnp.where(row == dp, chance, 0.0), axis=0, keepdims=True)
-        picks = picks_of[g][:, :group].astype(F32)
+        local = jnp.sum(jnp.where(row == dp, chance, 0.0), axis=0, keepdims=True)
+        picks = picks_of[g, :, lanes].astype(F32)
         named = jnp.logical_and(jnp.logical_or(row == experts, row == experts + 1), picks == dp.astype(F32))
         hit = jnp.sum(jnp.where(named, 1.0, 0.0), axis=0, keepdims=True)
-        scale = own.astype(BF16).astype(F32) * hit
-        column = jnp.transpose(jnp.broadcast_to(scale, (128, group)))[:, :1]
-        acted = jax.nn.gelu(pre[g], approximate=True)
-        hidden[g] = (acted * column).astype(BF16)
+        scale = local.astype(BF16).astype(F32) * hit
+        column = jnp.transpose(jnp.broadcast_to(scale, (128, half)))[:, :1]
+        acted = jax.nn.gelu(pre[g, rows[h]], approximate=True)
+        hidden[g, rows[h]] = (acted * column).astype(BF16)
 
     def product(g, zz, kk):
         cols = pl.ds(pl.multiple_of((zz * 2 + kk) * width, width), width)
@@ -414,9 +448,10 @@
     order = [
         (gx, slot(3)), (gy, slot(3)), (gd, passed(1)),
         (gx, slot(2)), (gy, slot(2)), (gd, passed(0)), (gd, turned(1)),
-        (dp, slot(3)), (gd, turned(0)),
-        (gx, slot(1)), (gy, slot(1)), (dp, slot(2)),
-        (dp, slot(1)), (gx, slot(0)), (gy, slot(0)), (dp, slot(0)),
+        (gd, turned(0)), (dp, slot(3)),
+        (gx, slot(1)), (gy, slot(1)),
+        (dp, slot(2)), (dp, slot(1)),
+        (gx, slot(0)), (gy, slot(0)), (dp, slot(0)),
     ]
 
     def lend(n, g, zz):
@@ -425,6 +460,62 @@
 
     def keep(g, zz):
         part[zz, g] = (product(g, zz, k) + take[zz, g].astype(F32)).astype(BF16)
+
+    def half_product(g, zz, kk, h):
+        cols = pl.ds(pl.multiple_of((zz * 2 + kk) * width, width), width)
+        return jnp.dot(hidden[g, rows[h]], wout[:, cols], preferred_element_type=F32)
+
+    def lend_half(n, h):
+        g, zz = order[n]
+        give[zz, g, rows[h]] = half_product(g, zz, 1 - k, h).astype(BF16)
+        send(give.at[zz, g, rows[h]], take.at[zz, g, rows[h]], ths.at[n, h], thr.at[n, h], partner)
+
+    def keep_half(n, h):
+        g, zz = order[n]
+        got(take.at[zz, g, rows[h]], ths.at[n, h], thr.at[n, h])
+        part[zz, g, rows[h]] = (half_product(g, zz, k, h) + take[zz, g, rows[h]].astype(F32)).astype(BF16)
+
+    def two(ref, h):
+        return jnp.concatenate([ref[gx, rows[h]], ref[gy, rows[h]]], axis=0)
+
+    def ready_two(h):
+        zz = slot(3)
+        for n, g in enumerate((gx, gy)):
+            got(xs.at[g, zz, 1 - k, rows[h]], hs.at[n, h], hr.at[n, h])
+        lanes = slice(h * half, h * half + half)
+        total = two(pre, h)
+        score = jnp.concatenate([logit[gx, :, lanes], logit[gy, :, lanes]], axis=1)
+        for kk in range(2):
+            strip = pl.ds(pl.multiple_of((zz * 2 + kk) * width, width), width)
+            block = jnp.concatenate([xs[gx, zz, kk, rows[h]], xs[gy, zz, kk, rows[h]]], axis=0)
+            total += jnp.dot(block, win[strip, :], preferred_element_type=F32)
+            score += lax.dot_general(gates[zz, kk], block, (((1,), (1,)), ((), ())), preferred_element_type=F32)
+        for n, g in enumerate((gx, gy)):
+            pre[g, rows[h]] = total[n * half:(n + 1) * half]
+            logit[g, :, lanes] = score[:, n * half:(n + 1) * half]
+            activate(g, h)
+        cols = pl.ds(pl.multiple_of((zz * 2 + 1 - k) * width, width), width)
+        lent = jnp.dot(two(hidden, h), wout[:, cols], preferred_element_type=F32).astype(BF16)
+        for n, g in enumerate((gx, gy)):
+            give[zz, g, rows[h]] = lent[n * half:(n + 1) * half]
+            send(give.at[zz, g, rows[h]], take.at[zz, g, rows[h]], ths.at[n, h], thr.at[n, h], partner)
+
+    def keep_two(h):
+        zz = slot(3)
+        cols = pl.ds(pl.multiple_of((zz * 2 + k) * width, width), width)
+        kept = jnp.dot(two(hidden, h), wout[:, cols], preferred_element_type=F32)
+        for n, g in enumerate((gx, gy)):
+            got(take.at[zz, g, rows[h]], ths.at[n, h], thr.at[n, h])
+            summed = kept[n * half:(n + 1) * half] + take[zz, g, rows[h]].astype(F32)
+            part[zz, g, rows[h]] = summed.astype(BF16)
+            to_side(3, n, h)
+
+    def ready(n, h):
+        g, zz = order[n]
+        got(xs.at[g, zz, 1 - k, rows[h]], hs.at[n, h], hr.at[n, h])
+        accumulate_half(g, zz, h)
+        activate(g, h)
+        lend_half(n, h)
 
     def lend_all(lo, hi):
         gs, zs = [w[0] for w in order[lo:hi]], [w[1] for w in order[lo:hi]]
@@ -440,13 +531,17 @@
         gs, zs = [w[0] for w in order[lo:hi]], [w[1] for w in order[lo:hi]]
         several(hi - lo, lambda c: keep(choose(c, gs), choose(c, zs)))
 
-    for n in range(len(order)):
+    for n in range(3, len(order)):
         g, zz = order[n]
         waits.append((None, make(give.at[zz, g], take.at[zz, g], ps.at[n], pr.at[n], partner)))
 
     def to_side(i, d, h):
         g = (gx, gy)[d]
         send(part.at[slot(i), g, rows[h]], from_side.at[i, d, h], side_s.at[i, d, h], side_r.at[i, d, h], side[d])
+
+    def to_pair_passed(j, h):
+        zz = passed(j)
+        send(part.at[zz, gd, rows[h]], from_pair.at[j, h], pair_s.at[j, h], pair_r.at[j, h], pair)
 
     def to_corner(j, h):
         zz = turned(j)
@@ -459,11 +554,6 @@
         for h, g in ((0, gy), (1, gx)):
             got(from_corner.at[j, h], corner_s.at[j, h], corner_r.at[j, h])
             part[zz, g, rows[h]] = (part[zz, g, rows[h]].astype(F32) + from_corner[j, h].astype(F32)).astype(BF16)
-
-    def send_passed(j):
-        zz = passed(j)
-        for h in range(2):
-            send(part.at[zz, gd, rows[h]], from_pair.at[j, h], pair_s.at[j, h], pair_r.at[j, h], pair)
 
     def gathered(i, h):
         total = part[slot(i), dp, rows[h]].astype(F32)
@@ -486,92 +576,105 @@
     def line_to_mid(i, h, n):
         return make(part.at[slot(i), dp, rows[h]], line_mid.at[n, h], lm_s.at[n, h], lm_r.at[n, h], across)
 
-    def settle(i):
-        for h in range(2):
-            total = gathered(i, h)
-            zz = slot(i)
-            to_pair_copy = line_to_pair(i, h, i - 1)
-
-            @pl.when(edge)
+    def settle(i, h):
+        total = gathered(i, h)
+        zz = slot(i)
+        to_pair_copy = line_to_pair(i, h, i - 1)
+
+        @pl.when(edge)
+        def _():
+            part[zz, dp, rows[h]] = total.astype(BF16)
+            to_pair_copy.start()
+
+        waits.append((edge, to_pair_copy))
+        if i == 3:
+
+            @pl.when(mid)
             def _():
                 part[zz, dp, rows[h]] = total.astype(BF16)
-                to_pair_copy.start()
-
-            waits.append((edge, to_pair_copy))
-            if i == 3:
-
-                @pl.when(mid)
-                def _():
-                    part[zz, dp, rows[h]] = total.astype(BF16)
-            else:
-                copy = line_to_mid(i, h, 2 - i)
-
-                @pl.when(mid)
-                def _():
-                    part[zz, dp, rows[h]] = (total + line_pair_in(i, h)).astype(BF16)
-                    copy.start()
-
-                waits.append((mid, copy))
-
-    def outer():
-        for h in range(2):
-            copy = line_to_pair(3, h, 0)
+        else:
+            copy = line_to_mid(i, h, 2 - i)
 
             @pl.when(mid)
             def _():
-                zz = slot(3)
-                came = line_mid_in(0, h)
-                part[zz, dp, rows[h]] = (part[zz, dp, rows[h]].astype(F32) + came).astype(BF16)
+                part[zz, dp, rows[h]] = (total + line_pair_in(i, h)).astype(BF16)
                 copy.start()
 
             waits.append((mid, copy))
 
+    def outer(h):
+        copy = line_to_pair(3, h, 0)
+
+        @pl.when(mid)
+        def _():
+            zz = slot(3)
+            came = line_mid_in(0, h)
+            part[zz, dp, rows[h]] = (part[zz, dp, rows[h]].astype(F32) + came).astype(BF16)
+            copy.start()
+
+        waits.append((mid, copy))
+
     load_out.wait()
-    for n, which in enumerate((from_x(3), from_y(3), from_passed(1))):
-        absorb(which)
-        activate(which[2])
-        lend(n, *order[n])
-    keep_all(0, 1)
-    for h in range(2):
-        to_side(3, 0, h)
-    keep_all(1, 2)
-    for h in range(2):
-        to_side(3, 1, h)
-    keep_all(2, 3)
-    send_passed(1)
-    activate(dp)
-    lend_all(3, 7)
-    keep_all(3, 7)
+    ready_two(0)
+    passed_in(1, 0)
+    cross_half(2, 0, gd, passed(1))
+    sides_in(3, 1)
+    cross_half(0, 1, gx, slot(3))
+    cross_half(1, 1, gy, slot(3))
+    ready(2, 0)
+    keep_two(0)
+    passed_in(1, 1)
+    cross_half(2, 1, gd, passed(1))
+    ready_two(1)
+    keep_half(2, 0)
+    to_pair_passed(1, 0)
+    ready(2, 1)
+    keep_two(1)
+    lend_all(3, 5)
+    keep_half(2, 1)
+    to_pair_passed(1, 1)
+    lend_all(5, 7)
+    keep_all(3, 5)
     to_side(2, 0, 0)
     to_side(2, 1, 1)
-    send_passed(0)
-    for h in range(2):
-        to_corner(1, h)
+    keep_all(5, 7)
+    to_pair_passed(0, 0)
+    to_pair_passed(0, 1)
+    to_corner(1, 0)
+    activate(dp, 0)
+    activate(dp, 1)
     lend_all(7, 9)
+    to_corner(1, 1)
+    lend_all(9, 11)
     keep_all(7, 9)
-    settle(3)
-    for h in range(2):
-        to_corner(0, h)
-    lend_all(9, 12)
+    settle(3, 0)
+    settle(3, 1)
+    lend_all(11, 13)
+    to_corner(0, 0)
+    keep_all(9, 11)
     pl.when(mid)(functools.partial(corner_add, 1))
+    to_side(2, 1, 0)
     to_side(2, 0, 1)
-    to_side(2, 1, 0)
-    keep_all(9, 12)
+    to_corner(0, 1)
     pl.when(edge)(functools.partial(corner_add, 1))
     to_side(1, 0, 0)
+    lend_all(13, 16)
+    keep_all(11, 13)
+    pl.when(mid)(functools.partial(corner_add, 0))
+    to_side(1, 1, 0)
+    to_side(1, 0, 1)
     to_side(1, 1, 1)
-    lend_all(12, 16)
-    pl.when(mid)(functools.partial(corner_add, 0))
-    to_side(1, 0, 1)
-    to_side(1, 1, 0)
-    settle(2)
-    keep_all(12, 16)
+    keep_all(13, 16)
     pl.when(edge)(functools.partial(corner_add, 0))
     for h in range(2):
         to_side(0, 0, h)
         to_side(0, 1, h)
-    settle(1)
-    outer()
+    settle(2, 0)
+    settle(2, 1)
+    outer(0)
+    settle(1, 0)
+    settle(1, 1)
+    outer(1)
     for h in range(2):
         total = gathered(0, h)
 
@@ -601,10 +704,12 @@
     return pl.pallas_call(
         functools.partial(whole_kernel, experts),
         out_shape=jax.ShapeDtypeStruct((group, width), BF16),
-        in_specs=[pl.BlockSpec(memory_space=vmem)] * 3 + [pl.BlockSpec(memory_space=pl.ANY)] * 2,
+        in_specs=[pl.BlockSpec(memory_space=pl.ANY)] * 5,
         out_specs=pl.BlockSpec(memory_space=vmem),
         scratch_shapes=[
             vmem((8, width), BF16),
+            vmem((experts, width), BF16),
+            vmem((2, group), jnp.int32),
             vmem((4, depth, 2, group, width), BF16),
             vmem((depth, 2, 8, width), BF16),
             vmem((4, 8, width), BF16),
@@ -621,7 +726,7 @@
             vmem((2, 2, half, width), BF16),
             vmem((3, 2, half, width), BF16),
             vmem((2, 2, half, width), BF16),
-            dma((2,)),
+            dma((5,)),
             dma((depth, 2, 2)), dma((depth, 2, 2)),
             dma((2, 2)), dma((2, 2)),
             dma((3, 2)), dma((2, 2)), dma((3, 2)),
@@ -631,6 +736,7 @@
             dma((3,)), dma((2,)), dma((3,)),
             dma((depth,)), dma((depth,)),
             dma((4 * depth,)), dma((4 * depth,)),
+            dma((3, 2)), dma((3, 2)), dma((3, 2)), dma((3, 2)),
             dma((depth, 2, 2)), dma((depth, 2, 2)),
             dma((2, 2)), dma((2, 2)),
             dma((2, 2)), dma((2, 2)),

time: 83.5 us -> 79.8 us (0.956)
  Pallas kernels: 81.6 us -> 78 us
    pallas_call x1, Pallas kernels: 81.6 us -> 78 us  [tokens_plan(): pl.pallas_call(functools.partial(whole_kernel, experts), out_shape=jax.Sh...]
where the time goes in v2:
time: 79.8 us; the launch traced here: 79.7 us
  Pallas kernels  78 us (98%)
  local copies, waits for them, and re-layouts  1.67 us (2%)
    pallas_call x1, Pallas kernels, tokens_plan(): pl.pallas_call(functools.partial(whole_kernel, experts), out_shape=jax.Sh...  78 us
    unnamed x1, local copies, waits for them, and re-layouts  1.67 us

profile of v2, /device:TPU:0, one launch (start us, length us, event | category | flops | bytes accessed | tf_op | source)
XLA Modules:
  0.0 79.7 jit_solution(15822877724312471647)
XLA Ops:
  0.0 78.0 %shard_map.55 = bf16[256,512]{1,0:T(8,128)(2,1)} custom-call(bf16[256,512]{1,0:T(8,128)(2,1)} %tok_hbm.1, bf16[4,512]{1,0:T(4,128)(2,1)} %bitcast.2, s32[2,256]{1,0:T(2,128)} %bitcast.3, bf16[1,4096,1024]{2,1,0:T(8,128)(2,1)} %win_hbm.1, bf16[1,1024,4096]{2,1,0:T(8,128)(2,1)} %wout_hbm.1), custom_call_target="tpu_custom_call" | custom-call | tf_op jit(solution)/shard_map/pallas_call | solution.py:704
  78.0 1.7 %copy.7 = bf16[256,512]{1,0:T(8,128)(2,1)} copy(bf16[256,512]{1,0:T(8,128)(2,1)} %shard_map.55) | data formatting | bytes 524288

commit v3 on v2

--- a/solution.py
+++ b/solution.py
@@ -90,7 +90,7 @@
     from_side, from_corner, from_pair, line_pair, line_mid,
     wsem, xy_s, xy_r, relay_s, relay_r, zp_s, zm_s, z_r, pass_s, pass_r, ds, dr,
     es, er, ep_s, em_s, ez_r, eds, edr,
-    ps, pr, hs, hr, ths, thr, side_s, side_r, corner_s, corner_r, pair_s, pair_r, lp_s, lp_r, lm_s, lm_r,
+    ps, pr, hs, hr, ths, thr, side_s, side_r, corner_s, corner_r, pair_s, pair_r, lp_s, lp_r, lm_s, lm_r, far_s, far_r, end_s, end_r,
 ):
     dp, me = lax.axis_index("dp"), lax.axis_index("expert")
     z, k = me // 2, me % 2
@@ -119,7 +119,7 @@
 
     pair, across = (dp, at(1 - near) * 2 + k), (dp, (depth - 1 - z) * 2 + k)
     side = ((gx, me), (gy, me))
-    waits = []
+    waits, late = [], []
 
     def make(src, dst, s_sem, r_sem, who):
         return pltpu.make_async_remote_copy(src, dst, s_sem, r_sem, device_id=who, device_id_type=MESH)
@@ -133,6 +133,16 @@
         copy = make(src, dst, s_sem, r_sem, who)
         pl.when(role)(copy.start)
         waits.append((role, copy))
+
+    def drain(copies):
+        for copy in [c for role, c in copies if role is None]:
+            copy.wait_send()
+        for which in (edge, mid):
+
+            @pl.when(which)
+            def _():
+                for copy in [c for role, c in copies if role is which]:
+                    copy.wait_send()
 
     def got(ref, s_sem, r_sem):
         make(ref, ref, s_sem, r_sem, partner).wait_recv()
@@ -408,7 +418,7 @@
     sides_in(3, 0)
     cross_half(0, 0, gx, slot(3))
     cross_half(1, 0, gy, slot(3))
-    absorb(from_turned(1), from_passed(0))
+    absorb(from_turned(1))
     for n in range(2 * depth):
         for d in range(2):
             waits.append((None, make(own.at[rows[0]], own.at[rows[0]], xy_s.at[n // 2, d, n % 2], xy_r.at[0, 0, 0], side[d])))
@@ -537,7 +547,12 @@
 
     def to_side(i, d, h):
         g = (gx, gy)[d]
-        send(part.at[slot(i), g, rows[h]], from_side.at[i, d, h], side_s.at[i, d, h], side_r.at[i, d, h], side[d])
+        make(part.at[slot(i), g, rows[h]], from_side.at[i, d, h], side_s.at[i, d, h], side_r.at[i, d, h], side[d]).start()
+
+    for n in range(4 * depth):
+        i, d, h = n // 4, n // 2 % 2, n % 2
+        kept = make(own.at[rows[0]], own.at[rows[0]], side_s.at[i, d, h], side_r.at[i, d, h], side[d])
+        (late if i < 2 else waits).append((None, kept))
 
     def to_pair_passed(j, h):
         zz = passed(j)
@@ -549,11 +564,10 @@
         part[zz, gd, rows[h]] = (part[zz, gd, rows[h]].astype(F32) + from_pair[j, h].astype(F32)).astype(BF16)
         send(part.at[zz, gd, rows[h]], from_corner.at[j, h], corner_s.at[j, h], corner_r.at[j, h], side[h])
 
-    def corner_add(j):
-        zz = turned(j)
-        for h, g in ((0, gy), (1, gx)):
-            got(from_corner.at[j, h], corner_s.at[j, h], corner_r.at[j, h])
-            part[zz, g, rows[h]] = (part[zz, g, rows[h]].astype(F32) + from_corner[j, h].astype(F32)).astype(BF16)
+    def corner_add(j, h):
+        zz, g = turned(j), (gy, gx)[h]
+        got(from_corner.at[j, h], corner_s.at[j, h], corner_r.at[j, h])
+        part[zz, g, rows[h]] = (part[zz, g, rows[h]].astype(F32) + from_corner[j, h].astype(F32)).astype(BF16)
 
     def gathered(i, h):
         total = part[slot(i), dp, rows[h]].astype(F32)
@@ -576,53 +590,68 @@
     def line_to_mid(i, h, n):
         return make(part.at[slot(i), dp, rows[h]], line_mid.at[n, h], lm_s.at[n, h], lm_r.at[n, h], across)
 
-    def settle(i, h):
+    fine = half // 2
+
+    def strip_of(h, c):
+        return pl.ds(h * half + c * fine, fine)
+
+    def far_to_mid(h, c):
+        n = 2 * h + c
+        piece = line_mid.at[0, h, pl.ds(c * fine, fine)]
+        return make(part.at[slot(2), dp, strip_of(h, c)], piece, far_s.at[n], far_r.at[n], across)
+
+    def far_to_edge(h, c):
+        n = 2 * h + c
+        piece = line_pair.at[0, h, pl.ds(c * fine, fine)]
+        return make(part.at[slot(3), dp, strip_of(h, c)], piece, end_s.at[n], end_r.at[n], pair)
+
+    def far_in(h, c):
+        got(line_mid.at[0, h, pl.ds(c * fine, fine)], far_s.at[0], far_r.at[2 * h + c])
+
+    def end_in(h, c):
+        got(line_pair.at[0, h, pl.ds(c * fine, fine)], end_s.at[0], end_r.at[2 * h + c])
+
+    def settle_edge(i, h):
+        part[slot(i), dp, rows[h]] = gathered(i, h).astype(BF16)
+        line_to_pair(i, h, i - 1).start()
+
+    def settle_mid(i, h):
         total = gathered(i, h)
-        zz = slot(i)
-        to_pair_copy = line_to_pair(i, h, i - 1)
-
-        @pl.when(edge)
-        def _():
-            part[zz, dp, rows[h]] = total.astype(BF16)
-            to_pair_copy.start()
-
-        waits.append((edge, to_pair_copy))
-        if i == 3:
-
-            @pl.when(mid)
-            def _():
-                part[zz, dp, rows[h]] = total.astype(BF16)
+        part[slot(i), dp, rows[h]] = (total + line_pair_in(i, h)).astype(BF16)
+        if i == 1:
+            line_to_mid(1, h, 1).start()
         else:
-            copy = line_to_mid(i, h, 2 - i)
-
-            @pl.when(mid)
-            def _():
-                part[zz, dp, rows[h]] = (total + line_pair_in(i, h)).astype(BF16)
-                copy.start()
-
-            waits.append((mid, copy))
+            for c in range(2):
+                far_to_mid(h, c).start()
+
+    for n in range(6):
+        i, h = n // 2 + 1, n % 2
+        late.append((edge, line_to_pair(i, h, i - 1)))
+        if i == 1:
+            late.append((mid, line_to_mid(1, h, 1)))
 
     def outer(h):
-        copy = line_to_pair(3, h, 0)
-
-        @pl.when(mid)
-        def _():
-            zz = slot(3)
-            came = line_mid_in(0, h)
-            part[zz, dp, rows[h]] = (part[zz, dp, rows[h]].astype(F32) + came).astype(BF16)
-            copy.start()
-
-        waits.append((mid, copy))
+        for c in range(2):
+            far_in(h, c)
+            strip = strip_of(h, c)
+            came = line_mid[0, h, c * fine:(c + 1) * fine].astype(F32)
+            part[slot(3), dp, strip] = (part[slot(3), dp, strip].astype(F32) + came).astype(BF16)
+            far_to_edge(h, c).start()
+
+    for n in range(4):
+        late.append((mid, far_to_mid(n // 2, n % 2)))
+        late.append((mid, far_to_edge(n // 2, n % 2)))
 
     load_out.wait()
     ready_two(0)
-    passed_in(1, 0)
-    cross_half(2, 0, gd, passed(1))
     sides_in(3, 1)
     cross_half(0, 1, gx, slot(3))
     cross_half(1, 1, gy, slot(3))
+    passed_in(1, 0)
+    cross_half(2, 0, gd, passed(1))
+    absorb(from_passed(0))
+    keep_two(0)
     ready(2, 0)
-    keep_two(0)
     passed_in(1, 1)
     cross_half(2, 1, gd, passed(1))
     ready_two(1)
@@ -630,13 +659,18 @@
     to_pair_passed(1, 0)
     ready(2, 1)
     keep_two(1)
-    lend_all(3, 5)
+    lend_all(3, 7)
     keep_half(2, 1)
     to_pair_passed(1, 1)
-    lend_all(5, 7)
     keep_all(3, 5)
     to_side(2, 0, 0)
     to_side(2, 1, 1)
+
+    @pl.when(edge)
+    def _():
+        to_side(2, 0, 1)
+        to_side(2, 1, 0)
+
     keep_all(5, 7)
     to_pair_passed(0, 0)
     to_pair_passed(0, 1)
@@ -647,34 +681,87 @@
     to_corner(1, 1)
     lend_all(9, 11)
     keep_all(7, 9)
-    settle(3, 0)
-    settle(3, 1)
+
+    @pl.when(edge)
+    def _():
+        settle_edge(3, 0)
+        settle_edge(3, 1)
+
+    @pl.when(mid)
+    def _():
+        for h in range(2):
+            part[slot(3), dp, rows[h]] = gathered(3, h).astype(BF16)
+
     lend_all(11, 13)
     to_corner(0, 0)
     keep_all(9, 11)
-    pl.when(mid)(functools.partial(corner_add, 1))
-    to_side(2, 1, 0)
-    to_side(2, 0, 1)
+
+    @pl.when(mid)
+    def _():
+        corner_add(1, 0)
+        to_side(2, 1, 0)
+        corner_add(1, 1)
+        to_side(2, 0, 1)
+
     to_corner(0, 1)
-    pl.when(edge)(functools.partial(corner_add, 1))
     to_side(1, 0, 0)
+    pl.when(edge)(functools.partial(to_side, 1, 1, 1))
     lend_all(13, 16)
     keep_all(11, 13)
-    pl.when(mid)(functools.partial(corner_add, 0))
-    to_side(1, 1, 0)
-    to_side(1, 0, 1)
-    to_side(1, 1, 1)
+
+    @pl.when(edge)
+    def _():
+        settle_edge(2, 0)
+        settle_edge(2, 1)
+
+    for role, j in ((edge, 1), (mid, 0)):
+
+        @pl.when(role)
+        def _():
+            corner_add(j, 0)
+            to_side(1, 1, 0)
+
+    @pl.when(edge)
+    def _():
+        corner_add(1, 1)
+        to_side(1, 0, 1)
+
+    @pl.when(mid)
+    def _():
+        to_side(1, 1, 1)
+
     keep_all(13, 16)
-    pl.when(edge)(functools.partial(corner_add, 0))
+
+    @pl.when(mid)
+    def _():
+        settle_mid(2, 0)
+        settle_mid(2, 1)
+        corner_add(0, 1)
+        to_side(1, 0, 1)
+
+    @pl.when(edge)
+    def _():
+        corner_add(0, 0)
+        corner_add(0, 1)
+
     for h in range(2):
         to_side(0, 0, h)
         to_side(0, 1, h)
-    settle(2, 0)
-    settle(2, 1)
-    outer(0)
-    settle(1, 0)
-    settle(1, 1)
-    outer(1)
+
+    drain(waits)
+
+    @pl.when(edge)
+    def _():
+        settle_edge(1, 0)
+        settle_edge(1, 1)
+
+    @pl.when(mid)
+    def _():
+        settle_mid(1, 0)
+        outer(0)
+        settle_mid(1, 1)
+        outer(1)
+
     for h in range(2):
         total = gathered(0, h)
 
@@ -684,13 +771,11 @@
 
         @pl.when(edge)
         def _():
-            out[rows[h]] = (total + line_pair_in(0, h)).astype(BF16)
-
-    for role, copy in waits:
-        if role is None:
-            copy.wait_send()
-        else:
-            pl.when(role)(copy.wait_send)
+            for c in range(2):
+                end_in(h, c)
+            out[rows[h]] = (total + line_pair[0, h].astype(F32)).astype(BF16)
+
+    drain(late)
 
 
 def tokens_plan(tokens, routing, gate_weight, expert_in, expert_out):
@@ -742,6 +827,7 @@
             dma((2, 2)), dma((2, 2)),
             dma((3, 2)), dma((3, 2)),
             dma((2, 2)), dma((2, 2)),
+            dma((4,)), dma((4,)), dma((4,)), dma((4,)),
         ],
         compiler_params=pltpu.CompilerParams(
             collective_id=0, has_side_effects=True, vmem_limit_bytes=63 * 1024 * 1024

time: 79.8 us -> 76.1 us (0.954)
  Pallas kernels: 78 us -> 74.3 us
    pallas_call x1, Pallas kernels: 78 us -> 74.3 us  [tokens_plan(): pl.pallas_call(functools.partial(whole_kernel, experts), out_shape=jax.Sh...]
where the time goes in v3:
time: 76.1 us; the launch traced here: 75.9 us
  Pallas kernels  74.3 us (98%)
  local copies, waits for them, and re-layouts  1.67 us (2%)
    pallas_call x1, Pallas kernels, tokens_plan(): pl.pallas_call(functools.partial(whole_kernel, experts), out_shape=jax.Sh...  74.3 us
    unnamed x1, local copies, waits for them, and re-layouts  1.67 us

profile of v3, /device:TPU:0, one launch (start us, length us, event | category | flops | bytes accessed | tf_op | source)
XLA Modules:
  0.0 75.9 jit_solution(113981140389189441)
XLA Ops:
  0.0 74.3 %shard_map.55 = bf16[256,512]{1,0:T(8,128)(2,1)} custom-call(bf16[256,512]{1,0:T(8,128)(2,1)} %tok_hbm.1, bf16[4,512]{1,0:T(4,128)(2,1)} %bitcast.2, s32[2,256]{1,0:T(2,128)} %bitcast.3, bf16[1,4096,1024]{2,1,0:T(8,128)(2,1)} %win_hbm.1, bf16[1,1024,4096]{2,1,0:T(8,128)(2,1)} %wout_hbm.1), custom_call_target="tpu_custom_call" | custom-call | tf_op jit(solution)/shard_map/pallas_call | solution.py:789
  74.3 1.7 %copy.7 = bf16[256,512]{1,0:T(8,128)(2,1)} copy(bf16[256,512]{1,0:T(8,128)(2,1)} %shard_map.55) | data formatting | bytes 524288
